TPU v7x, 128 devices: a whole 4x4x4 slice. The times are simulated.
128 devices in a mesh: seq: 32 (over z, y, x_hi), dp: 4 (over x_lo, core).
Axes of the slice: x: 4 (x_hi: 2, x_lo: 2; x = x_hi * 2 + x_lo), y: 4, z: 4, core: 2. Of those that a mesh axis runs over, the one named last changes fastest.
Arguments:
- hidden: bfloat16 [4, 8192, 4608], P('dp', 'seq'), may hold values from -6 to 6
- queries: bfloat16 [4, 8192, 2048], P('dp', 'seq'), may hold values from -64 to 64
- down_weight: bfloat16 [4608, 1024], P('dp'), may hold values from -0.09375 to 0.09375
- up_weight: bfloat16 [2, 512, 1024], P(None, 'dp'), may hold values from -0.25 to 0.25
- lengths: int32 [4], P('dp'), may hold values from 2048 to 8192
Outputs:
- latent_cache: bfloat16 [4, 8192, 1024], P('dp', 'seq')
- attended: bfloat16 [4, 8192, 2048], P('dp', 'seq')
All inputs are finite; a program needn't handle non-finite values.
Results may differ from a plain program's by a relative error of at most 0.012.
The roundings to bfloat16 on the way count: a program that leaves them out, or rounds other values in their place, can miss the bound.
Values may be sent and summed in bfloat16 or wider, within the bound.
No kernel may reach another device: no remote copies, remote signals or barrier semaphores. Data moves between devices by JAX's collectives and lax.ppermute only.
A program may use at most 128 MiB of HBM per device.

v0:
```python
import jax
import jax.numpy as jnp
from jax import lax
from jax.sharding import Mesh
from jax.sharding import PartitionSpec as P

HEAD = 128
WINDOW = 4096
DP = ("dp_0", "dp_1")
query_scale = 144.0 ** (-0.5)
soft_cap = 50.0


def laid_out(pieces, dim):
    lengths = list(pieces.shape[1:])
    lengths[dim] *= pieces.shape[0]
    return jnp.moveaxis(pieces, 0, dim).reshape(lengths)


def stacked_from(array, axes, turns):
    pieces = array
    for k in turns:
        pieces = lax.all_gather(pieces, axes[k])
    done = turns[::-1]
    back = [done.index(k) for k in range(len(axes))]
    pieces = pieces.transpose(*back, *range(len(axes), pieces.ndim))
    return pieces.reshape(-1, *array.shape)


def gathered_by_axis(array, axes, turns, dim):
    return laid_out(stacked_from(array, axes, turns), dim)


def from_everyone(array, axis):
    size = lax.axis_size(axis)
    return lax.all_to_all(
        jnp.broadcast_to(array[None], (size, *array.shape)), axis, 0, 0, tiled=True
    )


def gathered_copies(array, axis, dim):
    return laid_out(from_everyone(array, axis), dim)


def rotate(values_in, start_pos):
    batches, count, width = values_in.shape
    half_head = HEAD // 2
    places = (start_pos + jnp.arange(count, dtype=jnp.int32)).astype(jnp.float32)
    freqs = 10000.0 ** (-2.0 * jnp.arange(half_head, dtype=jnp.float32) / HEAD)
    angles = places[:, None] * freqs[None, :]
    cosine = jnp.cos(angles)[None, :, None, :]
    sine_val = jnp.sin(angles)[None, :, None, :]
    split_heads = values_in.reshape(batches, count, width // HEAD, 2, half_head)
    lower = split_heads[:, :, :, 0, :]
    upper = split_heads[:, :, :, 1, :]
    turned = jnp.stack(
        [lower * cosine - upper * sine_val, upper * cosine + lower * sine_val], axis=3
    )
    return turned.reshape(batches, count, width)


def expand(latent_rows, start_pos, uppers):
    batches, count, latent_rank = latent_rows.shape
    key_rank = latent_rank // 2
    kv_width = uppers.shape[2]
    keys_raw = jnp.dot(
        latent_rows[:, :, :key_rank].reshape(-1, key_rank),
        uppers[0],
        preferred_element_type=jnp.float32,
    )
    keys_out = rotate(keys_raw.reshape(batches, count, kv_width), start_pos).astype(jnp.bfloat16)
    values_out = jnp.dot(
        latent_rows[:, :, key_rank:].reshape(-1, key_rank),
        uppers[1],
        preferred_element_type=jnp.float32,
    )
    values_out = values_out.astype(jnp.bfloat16).reshape(batches, count, kv_width)
    return jnp.stack([keys_out, values_out])


def attend(state, pairs, start_pos, q_split, q_pos):
    numer, denom = state
    batches, count, kv_width = pairs.shape[1:]
    groups = kv_width // HEAD
    keys_grp = pairs[0].reshape(batches, count, groups, HEAD)
    values_grp = pairs[1].reshape(batches, count, groups, HEAD)
    raw = jnp.einsum("blgrd,bngd->bgrln", q_split, keys_grp, preferred_element_type=jnp.float32)
    capped = soft_cap * jnp.tanh(raw * (query_scale / soft_cap))
    key_pos = start_pos + jnp.arange(count, dtype=jnp.int32)
    allowed = (
        (key_pos[None, :] <= q_pos[:, None])
        & (key_pos[None, :] > q_pos[:, None] - WINDOW)
        & (key_pos[None, :] >= 0)
    )
    expo = jnp.where(allowed, jnp.exp(capped), 0.0)
    denom = denom + jnp.sum(expo, axis=-1)
    numer = numer + jnp.einsum(
        "bgrln,bngd->blgrd",
        expo.astype(jnp.bfloat16),
        values_grp,
        preferred_element_type=jnp.float32,
    )
    return (numer, denom)


def body(hidden, queries, down_weight, up_weight, lengths):
    seq_count, local_rows, model_dim = hidden.shape
    latent_rank = down_weight.shape[1]
    flat_hidden = hidden.reshape(seq_count * local_rows, model_dim)
    latent_sum = jnp.dot(
        flat_hidden,
        gathered_by_axis(down_weight, DP, (0, 1), 0),
        preferred_element_type=jnp.float32,
    )
    seq_index = lax.axis_index("seq")
    own_start = seq_index * local_rows
    q_pos = own_start + jnp.arange(local_rows, dtype=jnp.int32)
    is_live = q_pos[None, :] < lengths[:, None]
    latent = latent_sum.astype(jnp.bfloat16).reshape(seq_count, local_rows, latent_rank)
    latent = jnp.where(is_live[:, :, None], latent, jnp.zeros((), jnp.bfloat16))
    uppers = gathered_copies(up_weight, DP, 1)
    groups = up_weight.shape[2] // HEAD
    ratio = queries.shape[2] // (groups * HEAD)
    q_split = queries.reshape(seq_count, local_rows, groups, ratio, HEAD)
    initial = (
        jnp.zeros((seq_count, local_rows, groups, ratio, HEAD), jnp.float32),
        jnp.zeros((seq_count, groups, ratio, local_rows), jnp.float32),
    )

    def unpack(travel, start_pos):
        return expand(travel, start_pos, uppers)

    tile_rows = local_rows * max(1, 512 // local_rows)
    part = lax.all_gather(latent, "seq", axis=1, tiled=True)
    row_axis = part.ndim - 2
    count = part.shape[row_axis]
    pieces = count // tile_rows
    shaped = part.reshape(part.shape[:row_axis] + (pieces, tile_rows) + part.shape[row_axis + 1 :])
    shaped = jnp.moveaxis(shaped, row_axis, 0)

    def scan_step(inner, packed):
        offset, tile_data = packed
        tile_start = offset * tile_rows
        return (attend(inner, unpack(tile_data, tile_start), tile_start, q_split, q_pos), None)

    outcome = lax.scan(scan_step, initial, (jnp.arange(pieces, dtype=jnp.int32), shaped))
    numer, denom = outcome[0]
    result = numer / jnp.transpose(denom, (0, 3, 1, 2))[..., None]
    result = result.reshape(seq_count, local_rows, groups * ratio * HEAD)
    attended = jnp.where(is_live[:, :, None], result, 0.0).astype(jnp.bfloat16)
    return (latent, attended)


def solution(mesh):
    split = Mesh(mesh.devices.reshape(mesh.shape["seq"], 2, 2), ("seq", "dp_0", "dp_1"))
    placed = (P(DP, "seq", None), P(DP, "seq", None), P(DP, None), P(None, DP, None), P(DP))
    return jax.shard_map(
        body,
        mesh=split,
        in_specs=placed,
        out_specs=(P(DP, "seq", None), P(DP, "seq", None)),
        check_vma=False,
    )
```

profile of v0, /device:TPU:0, one launch (start us, length us, event | category | flops | bytes accessed | tf_op | source)
XLA Modules:
  0.0 543.6 jit_solution(10203643698651200933)
XLA Ops:
  8.0 69.3 %all-gather.7.cloned.1.call-done = bf16[2304,1024]{1,0:T(8,128)(2,1)} async-done(((bf16[1152,1024]{1,0:T(8,128)(2,1)}), bf16[2304,1024]{1,0:T(8,128)(2,1)}) %all-gather.7.cloned.1.call-update) | async-done | bytes 4718608 | tf_op jit(solution)/shard_map/all_gather | solution.py:23
  78.0 26.2 %all-gather.9.cloned.1.call-done = bf16[4,1152,1024]{2,1,0:T(8,128)(2,1)} async-done(((bf16[2,1152,1024]{2,1,0:T(8,128)(2,1)}), bf16[4,1152,1024]{2,1,0:T(8,128)(2,1)}) %all-gather.9.cloned.1.call-update) | async-done | bytes 9437200 | tf_op jit(solution)/shard_map/all_gather | solution.py:23
  104.3 8.4 %copy.42 = bf16[2,2,1152,1024]{3,2,1,0:T(8,128)(2,1)} copy(bf16[2,2,1152,1024]{3,2,0,1:T(8,128)(2,1)} %bitcast.131) | data formatting | bytes 18874368 | tf_op jit(solution)/shard_map/transpose | solution.py:26
  112.7 7.1 %fusion.24 = bf16[256,1024]{1,0:T(8,128)(2,1)} fusion(bf16[4608,1024]{1,0:T(8,128)(2,1)} %bitcast.132, bf16[1,256,4608]{2,1,0:T(8,128)(2,1)S(1)} %copy-done, pred[256]{0:T(512)(128)(4,1)S(1)} %add_compare_fusion), kind=kOutput, calls=%fused_computation.37 | convolution fusion | flops 2416443392 | bytes 12321024 | tf_op jit(solution)/shard_map/dot_general | solution.py:110
  121.8 3.6 all-to-all-start
  128.2 26.6 %all-to-all-done = bf16[4,2,128,1024]{2,3,1,0:T(8,128)(2,1)S(1)} async-done(((bf16[4,2,128,1024]{2,3,1,0:T(8,128)(2,1)}), bf16[4,2,128,1024]{2,3,1,0:T(8,128)(2,1)S(1)}, u32[]{:S(2)}, u32[]{:S(2)}) %all-to-all-start) | async-done | bytes 2097184 | tf_op jit(solution)/shard_map/all_to_all | solution.py:36
  157.5 4.0 copy.47
  161.5 120.0 %all-gather.11.cloned.1.call-done = bf16[8192,1024]{1,0:T(8,128)(2,1)} async-done(((bf16[256,1024]{1,0:T(8,128)(2,1)}), bf16[8192,1024]{1,0:T(8,128)(2,1)}) %all-gather.11.cloned.1.call-update) | async-done | bytes 16777232 | tf_op jit(solution)/shard_map/all_gather | solution.py:134
  281.5 249.8 %while.15 = (s32[]{:T(128)}, f32[1,256,8,2,128]{1,4,3,2,0:T(8,128)}, f32[1,8,2,256]{3,2,1,0:T(2,128)S(1)}, bf16[16,1,512,1024]{3,2,1,0:T(8,128)(2,1)}, bf16[2,51...) while((s32[]{:T(128)}, ...), condition=%wide.region_2.3_spmd.clone, body=%wide.region_0.2_spmd.clone.sunk | while | flops 2169018880 | bytes 72300888 | solution.py:146
  289.5 3.4 fusion.44
  305.1 3.4 fusion.44
  320.7 3.4 fusion.44
  336.3 3.4 fusion.44
  351.9 3.4 fusion.44
  367.5 3.4 fusion.44
  383.1 3.4 fusion.44
  398.7 3.4 fusion.44
  414.4 3.4 fusion.44
  430.0 3.4 fusion.44
  445.6 3.4 fusion.44
  461.2 3.4 fusion.44
  476.8 3.4 fusion.44
  492.4 3.4 fusion.44
  508.0 3.4 fusion.44
  (477 shorter events, 199.2 us)
Async XLA Ops:
  7.2 105.5 %copy-start = (bf16[1,256,4608]{2,1,0:T(8,128)(2,1)S(1)}, bf16[1,256,4608]{2,1,0:T(8,128)(2,1)}, u32[]{:S(2)}) copy-start(bf16[1,256,4608]{2,1,0:T(8,128)(2,1)} %param.7) | copy-start | bytes 7077892
  7.2 70.1 %all-gather.7.cloned.1.call-start = ((), (), s32[]{:S(2)}) async-start(), calls=%async_computation.1 | async-start | bytes 7077888 | tf_op jit(solution)/shard_map/all_gather | solution.py:23
  7.9 96.4 %all-gather.9.cloned.1.call-start = ((), (), s32[]{:S(2)}) async-start(), calls=%async_computation.2 | async-start | bytes 14155776 | tf_op jit(solution)/shard_map/all_gather | solution.py:23
  77.3 204.1 %all-gather.11.cloned.1.call-start = ((), (), s32[]{:S(2)}) async-start(), calls=%async_computation.3 | async-start | bytes 17301504 | tf_op jit(solution)/shard_map/all_gather | solution.py:134
  78.0 34.7 %copy-start.7 = (pred[256]{0:T(512)(128)(4,1)}, pred[256]{0:T(512)(128)(4,1)S(1)}, u32[]{:S(2)}) copy-start(pred[256]{0:T(512)(128)(4,1)S(1)} %add_compare_fusion) | copy-start | bytes 772
  112.7 7.2 %copy-start.6 = (bf16[2,128,1024]{2,1,0:T(8,128)(2,1)S(1)}, bf16[2,128,1024]{2,1,0:T(8,128)(2,1)}, u32[]{:S(2)}) copy-start(bf16[2,128,1024]{2,1,0:T(8,128)(2,1)} %param.10) | copy-start | bytes 1572868
  121.8 33.0 %all-to-all-start = ((bf16[4,2,128,1024]{2,3,1,0:T(8,128)(2,1)}), bf16[4,2,128,1024]{2,3,1,0:T(8,128)(2,1)S(1)}, u32[]{:S(2)}, u32[]{:S(2)}) async-start(bf16[4,2,128,1024]{2,3,1,0:T(8,128)(2,1)} %broadcast_in_dim.69), calls=%async_computation | async-start | bytes 4194304 | tf_op jit(solution)/shard_map/all_to_all | solution.py:36
  292.9 4.2 copy-start.10
  308.5 4.2 copy-start.10
  324.1 4.2 copy-start.10
  339.8 4.2 copy-start.10
  355.4 4.2 copy-start.10
  371.0 4.2 copy-start.10
  386.6 4.2 copy-start.10
  402.2 4.2 copy-start.10
  417.8 4.2 copy-start.10
  433.4 4.2 copy-start.10
  449.0 4.2 copy-start.10
  464.7 4.2 copy-start.10
  480.3 4.2 copy-start.10
  495.9 4.2 copy-start.10
  511.5 4.2 copy-start.10
  527.1 4.2 copy-start.10
  531.3 5.8 %copy-start.1 = (bf16[1,256,4608]{2,1,0:T(8,128)(2,1)S(1)}, bf16[1,256,4608]{2,1,0:T(8,128)(2,1)}, u32[]{:S(2)}) copy-start(bf16[1,256,4608]{2,1,0:T(8,128)(2,1)} %param.7) | copy-start | bytes 7077892
  (81 other events, 186.4 us)
Sparse Core Ops, SparseCore 0:
  9.6 67.6 all-gather.6
  79.0 25.2 all-gather.8
  120.0 161.4 all-gather.10
where the time goes:
time: 546 us; the launch traced here: 544 us
  waiting for transfers between devices  243 us (45%)
  matrix products  132 us (24%)
  local copies, waits for them, and re-layouts  113 us (21%)
  other arithmetic  24.6 us (5%)
  between operations  14.5 us (3%)
  loops' own time  13.1 us (2%)
    all_gather x1, waiting for transfers between devices, body(): part = lax.all_gather(latent, 'seq', axis=1, tiled=True)  120 us
    all_gather x2, waiting for transfers between devices, stacked_from(): pieces = lax.all_gather(pieces, axes[k])  95.6 us
    dot_general x16, matrix products, attend(): jnp.einsum('blgrd,bngd->bgrln', q_split, keys_grp, preferred_element_type...  55 us
    dot_general x16, matrix products, attend(): jnp.einsum('bgrln,bngd->blgrd', expo.astype(jnp.bfloat16), values_grp, pr...  45.5 us
    while x192, local copies, waits for them, and re-layouts  32.4 us
    all_to_all x1, waiting for transfers between devices, from_everyone(): lax.all_to_all(jnp.broadcast_to(array[None], (size, *array.shape)), axis,...  26.6 us
    squeeze x16, local copies, waits for them, and re-layouts, body(): lax.scan(scan_step, initial, (jnp.arange(pieces, dtype=jnp.int32), shaped))  20.8 us
    slice x16, local copies, waits for them, and re-layouts, expand(): uppers[0]  20.7 us
  transfers between devices with their start and end apart: 4, of which 4 were waited for; matrix products, arithmetic and copies ran while one was open for 2% of the time, Pallas kernels for 0%

commit v1 on v0

--- a/solution.py
+++ b/solution.py
@@ -131,7 +131,9 @@
         return expand(travel, start_pos, uppers)
 
     tile_rows = local_rows * max(1, 512 // local_rows)
-    part = lax.all_gather(latent, "seq", axis=1, tiled=True)
+    part = jnp.concatenate(
+        lax.all_to_all(jnp.stack([latent] * lax.axis_size("seq")), "seq", 0, 0), axis=1
+    )
     row_axis = part.ndim - 2
     count = part.shape[row_axis]
     pieces = count // tile_rows

time: 546 us -> 758 us (1.39)
  the two profiles are of different devices: /device:TPU:0 before, /device:TPU:60 now
where the time goes in v1:
time: 758 us; the launch traced here: 756 us
  waiting for transfers between devices  372 us (49%)
  matrix products  235 us (31%)
  local copies, waits for them, and re-layouts  84.4 us (11%)
  other arithmetic  24.5 us (3%)
  between operations  14.8 us (2%)
  starting transfers between devices  14.5 us (2%)
  loops' own time  10.9 us (1%)
    all_to_all x1, waiting for transfers between devices, body(): lax.all_to_all(jnp.stack([latent] * lax.axis_size('seq')), 'seq', 0, 0)  282 us
    dot_general x16, matrix products, attend(): jnp.einsum('bgrln,bngd->blgrd', expo.astype(jnp.bfloat16), values_grp, pr...  127 us
    all_gather x2, waiting for transfers between devices, stacked_from(): pieces = lax.all_gather(pieces, axes[k])  88.6 us
    dot_general x16, matrix products, attend(): jnp.einsum('blgrd,bngd->bgrln', q_split, keys_grp, preferred_element_type...  78.3 us
    squeeze x16, local copies, waits for them, and re-layouts, body(): lax.scan(scan_step, initial, (jnp.arange(pieces, dtype=jnp.int32), shaped))  20.8 us
    slice x16, local copies, waits for them, and re-layouts, expand(): uppers[0]  20.7 us
  transfers between devices with their start and end apart: 4, of which 3 were waited for; matrix products, arithmetic and copies ran while one was open for 3% of the time, Pallas kernels for 0%

profile of v1, /device:TPU:60, one launch (start us, length us, event | category | flops | bytes accessed | tf_op | source)
XLA Modules:
  0.0 755.7 jit_solution(16736941010433916315)
XLA Ops:
  8.0 68.3 %all-gather.5.cloned.1.call-done = bf16[2304,1024]{1,0:T(8,128)(2,1)} async-done(((bf16[1152,1024]{1,0:T(8,128)(2,1)}), bf16[2304,1024]{1,0:T(8,128)(2,1)}) %all-gather.5.cloned.1.call-update) | async-done | bytes 4718608 | tf_op jit(solution)/shard_map/all_gather | solution.py:23
  83.2 20.4 %all-gather.7.cloned.1.call-done = bf16[4,1152,1024]{2,1,0:T(8,128)(2,1)} async-done(((bf16[2,1152,1024]{2,1,0:T(8,128)(2,1)}), bf16[4,1152,1024]{2,1,0:T(8,128)(2,1)}) %all-gather.7.cloned.1.call-update) | async-done | bytes 9437200 | tf_op jit(solution)/shard_map/all_gather | solution.py:23
  103.6 8.5 %copy.39 = bf16[2,2,1152,1024]{3,2,1,0:T(8,128)(2,1)} copy(bf16[2,2,1152,1024]{3,2,0,1:T(8,128)(2,1)} %bitcast.131) | data formatting | bytes 18874368 | tf_op jit(solution)/shard_map/transpose | solution.py:26
  112.1 6.3 fusion.24
  118.4 6.1 stack.8
  124.5 10.0 %all-to-all-start = ((bf16[32,1,256,1024]{3,2,1,0:T(8,128)(2,1)}), bf16[32,1,256,1024]{3,2,1,0:T(8,128)(2,1)}, u32[]{:S(2)}, u32[]{:S(2)}) async-start(bf16[32,1,256,1024]{3,2,1,0:T(8,128)(2,1)} %stack.8), calls=%async_computation | async-start | bytes 33554432 | tf_op jit(solution)/shard_map/all_to_all | solution.py:135
  141.4 282.3 %all-to-all-done = bf16[32,1,256,1024]{3,2,1,0:T(8,128)(2,1)} async-done(((bf16[32,1,256,1024]{3,2,1,0:T(8,128)(2,1)}), bf16[32,1,256,1024]{3,2,1,0:T(8,128)(2,1)}, u32[]{:S(2)}, u32[]{:S(2)}) %all-to-all-start) | async-done | bytes 16777248 | tf_op jit(solution)/shard_map/all_to_all | solution.py:135
  423.7 319.4 %while.15 = (s32[]{:T(128)}, f32[1,256,8,2,128]{1,4,3,2,0:T(8,128)}, f32[1,8,2,256]{3,2,1,0:T(2,128)S(1)}, bf16[16,1,512,1024]{3,2,1,0:T(8,128)(2,1)}, bf16[2,51...) while((s32[]{:T(128)}, ...), condition=%wide.region_2.3_spmd.clone, body=%wide.region_0.2_spmd.clone.sunk | while | flops 2169018880 | bytes 51328696 | solution.py:148
  435.7 7.4 bitcast_add_fusion.4
  455.1 8.0 %bitcast_add_fusion.4 = f32[1,256,8,2,128]{1,4,3,2,0:T(8,128)} fusion(f32[1,256,8,2,128]{1,4,3,2,0:T(8,128)} %get-tuple-element.276, bf16[512,8,128,1]{0,2,3,1:T(8,128)(2,1)S(1)} %bitcast.130, f32[8,512,256,2]{2,1,3,0:T(8,128)} %get-tuple-element.262, pred[256,512]{0,1:T(8,128)(4,1)S(1)} %and_and_fusion.2, pred[]{:T(512)S(6)} %compare.3), kind=kOutput, calls=%fused_computation.7.clone.1 | convolution fusion | flops 546308096 | bytes 13762561 | tf_op jit(solution)/shard_map/while/body/eval_jaxpr/bgrln,bngd->blgrd/dot_general | solution.py:97
  475.1 8.0 %bitcast_add_fusion.4 = f32[1,256,8,2,128]{1,4,3,2,0:T(8,128)} fusion(f32[1,256,8,2,128]{1,4,3,2,0:T(8,128)} %get-tuple-element.276, bf16[512,8,128,1]{0,2,3,1:T(8,128)(2,1)S(1)} %bitcast.130, f32[8,512,256,2]{2,1,3,0:T(8,128)} %get-tuple-element.262, pred[256,512]{0,1:T(8,128)(4,1)S(1)} %and_and_fusion.2, pred[]{:T(512)S(6)} %compare.3), kind=kOutput, calls=%fused_computation.7.clone.1 | convolution fusion | flops 546308096 | bytes 13762561 | tf_op jit(solution)/shard_map/while/body/eval_jaxpr/bgrln,bngd->blgrd/dot_general | solution.py:97
  495.1 8.0 %bitcast_add_fusion.4 = f32[1,256,8,2,128]{1,4,3,2,0:T(8,128)} fusion(f32[1,256,8,2,128]{1,4,3,2,0:T(8,128)} %get-tuple-element.276, bf16[512,8,128,1]{0,2,3,1:T(8,128)(2,1)S(1)} %bitcast.130, f32[8,512,256,2]{2,1,3,0:T(8,128)} %get-tuple-element.262, pred[256,512]{0,1:T(8,128)(4,1)S(1)} %and_and_fusion.2, pred[]{:T(512)S(6)} %compare.3), kind=kOutput, calls=%fused_computation.7.clone.1 | convolution fusion | flops 546308096 | bytes 13762561 | tf_op jit(solution)/shard_map/while/body/eval_jaxpr/bgrln,bngd->blgrd/dot_general | solution.py:97
  515.1 8.0 %bitcast_add_fusion.4 = f32[1,256,8,2,128]{1,4,3,2,0:T(8,128)} fusion(f32[1,256,8,2,128]{1,4,3,2,0:T(8,128)} %get-tuple-element.276, bf16[512,8,128,1]{0,2,3,1:T(8,128)(2,1)S(1)} %bitcast.130, f32[8,512,256,2]{2,1,3,0:T(8,128)} %get-tuple-element.262, pred[256,512]{0,1:T(8,128)(4,1)S(1)} %and_and_fusion.2, pred[]{:T(512)S(6)} %compare.3), kind=kOutput, calls=%fused_computation.7.clone.1 | convolution fusion | flops 546308096 | bytes 13762561 | tf_op jit(solution)/shard_map/while/body/eval_jaxpr/bgrln,bngd->blgrd/dot_general | solution.py:97
  535.1 8.0 %bitcast_add_fusion.4 = f32[1,256,8,2,128]{1,4,3,2,0:T(8,128)} fusion(f32[1,256,8,2,128]{1,4,3,2,0:T(8,128)} %get-tuple-element.276, bf16[512,8,128,1]{0,2,3,1:T(8,128)(2,1)S(1)} %bitcast.130, f32[8,512,256,2]{2,1,3,0:T(8,128)} %get-tuple-element.262, pred[256,512]{0,1:T(8,128)(4,1)S(1)} %and_and_fusion.2, pred[]{:T(512)S(6)} %compare.3), kind=kOutput, calls=%fused_computation.7.clone.1 | convolution fusion | flops 546308096 | bytes 13762561 | tf_op jit(solution)/shard_map/while/body/eval_jaxpr/bgrln,bngd->blgrd/dot_general | solution.py:97
  555.1 8.0 %bitcast_add_fusion.4 = f32[1,256,8,2,128]{1,4,3,2,0:T(8,128)} fusion(f32[1,256,8,2,128]{1,4,3,2,0:T(8,128)} %get-tuple-element.276, bf16[512,8,128,1]{0,2,3,1:T(8,128)(2,1)S(1)} %bitcast.130, f32[8,512,256,2]{2,1,3,0:T(8,128)} %get-tuple-element.262, pred[256,512]{0,1:T(8,128)(4,1)S(1)} %and_and_fusion.2, pred[]{:T(512)S(6)} %compare.3), kind=kOutput, calls=%fused_computation.7.clone.1 | convolution fusion | flops 546308096 | bytes 13762561 | tf_op jit(solution)/shard_map/while/body/eval_jaxpr/bgrln,bngd->blgrd/dot_general | solution.py:97
  575.1 8.0 %bitcast_add_fusion.4 = f32[1,256,8,2,128]{1,4,3,2,0:T(8,128)} fusion(f32[1,256,8,2,128]{1,4,3,2,0:T(8,128)} %get-tuple-element.276, bf16[512,8,128,1]{0,2,3,1:T(8,128)(2,1)S(1)} %bitcast.130, f32[8,512,256,2]{2,1,3,0:T(8,128)} %get-tuple-element.262, pred[256,512]{0,1:T(8,128)(4,1)S(1)} %and_and_fusion.2, pred[]{:T(512)S(6)} %compare.3), kind=kOutput, calls=%fused_computation.7.clone.1 | convolution fusion | flops 546308096 | bytes 13762561 | tf_op jit(solution)/shard_map/while/body/eval_jaxpr/bgrln,bngd->blgrd/dot_general | solution.py:97
  595.1 8.0 %bitcast_add_fusion.4 = f32[1,256,8,2,128]{1,4,3,2,0:T(8,128)} fusion(f32[1,256,8,2,128]{1,4,3,2,0:T(8,128)} %get-tuple-element.276, bf16[512,8,128,1]{0,2,3,1:T(8,128)(2,1)S(1)} %bitcast.130, f32[8,512,256,2]{2,1,3,0:T(8,128)} %get-tuple-element.262, pred[256,512]{0,1:T(8,128)(4,1)S(1)} %and_and_fusion.2, pred[]{:T(512)S(6)} %compare.3), kind=kOutput, calls=%fused_computation.7.clone.1 | convolution fusion | flops 546308096 | bytes 13762561 | tf_op jit(solution)/shard_map/while/body/eval_jaxpr/bgrln,bngd->blgrd/dot_general | solution.py:97
  615.1 8.0 %bitcast_add_fusion.4 = f32[1,256,8,2,128]{1,4,3,2,0:T(8,128)} fusion(f32[1,256,8,2,128]{1,4,3,2,0:T(8,128)} %get-tuple-element.276, bf16[512,8,128,1]{0,2,3,1:T(8,128)(2,1)S(1)} %bitcast.130, f32[8,512,256,2]{2,1,3,0:T(8,128)} %get-tuple-element.262, pred[256,512]{0,1:T(8,128)(4,1)S(1)} %and_and_fusion.2, pred[]{:T(512)S(6)} %compare.3), kind=kOutput, calls=%fused_computation.7.clone.1 | convolution fusion | flops 546308096 | bytes 13762561 | tf_op jit(solution)/shard_map/while/body/eval_jaxpr/bgrln,bngd->blgrd/dot_general | solution.py:97
  635.1 8.0 %bitcast_add_fusion.4 = f32[1,256,8,2,128]{1,4,3,2,0:T(8,128)} fusion(f32[1,256,8,2,128]{1,4,3,2,0:T(8,128)} %get-tuple-element.276, bf16[512,8,128,1]{0,2,3,1:T(8,128)(2,1)S(1)} %bitcast.130, f32[8,512,256,2]{2,1,3,0:T(8,128)} %get-tuple-element.262, pred[256,512]{0,1:T(8,128)(4,1)S(1)} %and_and_fusion.2, pred[]{:T(512)S(6)} %compare.3), kind=kOutput, calls=%fused_computation.7.clone.1 | convolution fusion | flops 546308096 | bytes 13762561 | tf_op jit(solution)/shard_map/while/body/eval_jaxpr/bgrln,bngd->blgrd/dot_general | solution.py:97
  655.1 8.0 %bitcast_add_fusion.4 = f32[1,256,8,2,128]{1,4,3,2,0:T(8,128)} fusion(f32[1,256,8,2,128]{1,4,3,2,0:T(8,128)} %get-tuple-element.276, bf16[512,8,128,1]{0,2,3,1:T(8,128)(2,1)S(1)} %bitcast.130, f32[8,512,256,2]{2,1,3,0:T(8,128)} %get-tuple-element.262, pred[256,512]{0,1:T(8,128)(4,1)S(1)} %and_and_fusion.2, pred[]{:T(512)S(6)} %compare.3), kind=kOutput, calls=%fused_computation.7.clone.1 | convolution fusion | flops 546308096 | bytes 13762561 | tf_op jit(solution)/shard_map/while/body/eval_jaxpr/bgrln,bngd->blgrd/dot_general | solution.py:97
  675.1 8.0 %bitcast_add_fusion.4 = f32[1,256,8,2,128]{1,4,3,2,0:T(8,128)} fusion(f32[1,256,8,2,128]{1,4,3,2,0:T(8,128)} %get-tuple-element.276, bf16[512,8,128,1]{0,2,3,1:T(8,128)(2,1)S(1)} %bitcast.130, f32[8,512,256,2]{2,1,3,0:T(8,128)} %get-tuple-element.262, pred[256,512]{0,1:T(8,128)(4,1)S(1)} %and_and_fusion.2, pred[]{:T(512)S(6)} %compare.3), kind=kOutput, calls=%fused_computation.7.clone.1 | convolution fusion | flops 546308096 | bytes 13762561 | tf_op jit(solution)/shard_map/while/body/eval_jaxpr/bgrln,bngd->blgrd/dot_general | solution.py:97
  695.1 8.0 %bitcast_add_fusion.4 = f32[1,256,8,2,128]{1,4,3,2,0:T(8,128)} fusion(f32[1,256,8,2,128]{1,4,3,2,0:T(8,128)} %get-tuple-element.276, bf16[512,8,128,1]{0,2,3,1:T(8,128)(2,1)S(1)} %bitcast.130, f32[8,512,256,2]{2,1,3,0:T(8,128)} %get-tuple-element.262, pred[256,512]{0,1:T(8,128)(4,1)S(1)} %and_and_fusion.2, pred[]{:T(512)S(6)} %compare.3), kind=kOutput, calls=%fused_computation.7.clone.1 | convolution fusion | flops 546308096 | bytes 13762561 | tf_op jit(solution)/shard_map/while/body/eval_jaxpr/bgrln,bngd->blgrd/dot_general | solution.py:97
  715.1 8.0 %bitcast_add_fusion.4 = f32[1,256,8,2,128]{1,4,3,2,0:T(8,128)} fusion(f32[1,256,8,2,128]{1,4,3,2,0:T(8,128)} %get-tuple-element.276, bf16[512,8,128,1]{0,2,3,1:T(8,128)(2,1)S(1)} %bitcast.130, f32[8,512,256,2]{2,1,3,0:T(8,128)} %get-tuple-element.262, pred[256,512]{0,1:T(8,128)(4,1)S(1)} %and_and_fusion.2, pred[]{:T(512)S(6)} %compare.3), kind=kOutput, calls=%fused_computation.7.clone.1 | convolution fusion | flops 546308096 | bytes 13762561 | tf_op jit(solution)/shard_map/while/body/eval_jaxpr/bgrln,bngd->blgrd/dot_general | solution.py:97
  735.1 8.0 %bitcast_add_fusion.4 = f32[1,256,8,2,128]{1,4,3,2,0:T(8,128)} fusion(f32[1,256,8,2,128]{1,4,3,2,0:T(8,128)} %get-tuple-element.276, bf16[512,8,128,1]{0,2,3,1:T(8,128)(2,1)S(1)} %bitcast.130, f32[8,512,256,2]{2,1,3,0:T(8,128)} %get-tuple-element.262, pred[256,512]{0,1:T(8,128)(4,1)S(1)} %and_and_fusion.2, pred[]{:T(512)S(6)} %compare.3), kind=kOutput, calls=%fused_computation.7.clone.1 | convolution fusion | flops 546308096 | bytes 13762561 | tf_op jit(solution)/shard_map/while/body/eval_jaxpr/bgrln,bngd->blgrd/dot_general | solution.py:97
  (317 shorter events, 201.6 us)
Async XLA Ops:
  7.2 104.9 %copy-start = (bf16[1,256,4608]{2,1,0:T(8,128)(2,1)S(1)}, bf16[1,256,4608]{2,1,0:T(8,128)(2,1)}, u32[]{:S(2)}) copy-start(bf16[1,256,4608]{2,1,0:T(8,128)(2,1)} %param.7) | copy-start | bytes 7077892
  7.2 69.1 %copy-start.5 = (bf16[2,128,1024]{2,1,0:T(8,128)(2,1)S(1)}, bf16[2,128,1024]{2,1,0:T(8,128)(2,1)}, u32[]{:S(2)}) copy-start(bf16[2,128,1024]{2,1,0:T(8,128)(2,1)} %param.10) | copy-start | bytes 1572868
  7.2 69.0 %all-gather.5.cloned.1.call-start = ((), (), s32[]{:S(2)}) async-start(), calls=%async_computation.2 | async-start | bytes 7077888 | tf_op jit(solution)/shard_map/all_gather | solution.py:23
  7.9 95.7 %all-gather.7.cloned.1.call-start = ((), (), s32[]{:S(2)}) async-start(), calls=%async_computation.3 | async-start | bytes 14155776 | tf_op jit(solution)/shard_map/all_gather | solution.py:23
  78.1 40.2 %all-to-all-start.1 = ((bf16[4,2,128,1024]{2,3,1,0:T(8,128)(2,1)}), bf16[4,2,128,1024]{2,3,1,0:T(8,128)(2,1)}, u32[]{:S(2)}, u32[]{:S(2)}) async-start(bf16[4,2,128,1024]{2,3,1,0:T(8,128)(2,1)} %broadcast_in_dim.69), calls=%async_computation.1 | async-start | bytes 4194304 | tf_op jit(solution)/shard_map/all_to_all | solution.py:36
  118.3 6.2 copy-start.4
  124.5 10.1 %copy-start.3 = (bf16[1,256,2048]{2,1,0:T(8,128)(2,1)S(1)}, bf16[1,256,2048]{2,1,0:T(8,128)(2,1)}, u32[]{:S(2)}) copy-start(bf16[1,256,2048]{2,1,0:T(8,128)(2,1)} %param.8) | copy-start | bytes 3145732
  124.5 299.2 %all-to-all-start = ((bf16[32,1,256,1024]{3,2,1,0:T(8,128)(2,1)}), bf16[32,1,256,1024]{3,2,1,0:T(8,128)(2,1)}, u32[]{:S(2)}, u32[]{:S(2)}) async-start(bf16[32,1,256,1024]{3,2,1,0:T(8,128)(2,1)} %stack.8), calls=%async_computation | async-start | bytes 33554432 | tf_op jit(solution)/shard_map/all_to_all | solution.py:135
  448.9 4.9 copy-start.2
  468.9 4.9 copy-start.2
  488.9 4.9 copy-start.2
  508.9 4.9 copy-start.2
  528.9 4.9 copy-start.2
  548.9 4.9 copy-start.2
  568.9 4.9 copy-start.2
  588.9 4.9 copy-start.2
  608.9 4.9 copy-start.2
  628.9 4.9 copy-start.2
  648.9 4.9 copy-start.2
  668.9 4.9 copy-start.2
  688.9 4.9 copy-start.2
  708.9 4.9 copy-start.2
  728.9 4.9 copy-start.2
  743.1 5.8 copy-start.1
  (1 other events, 4.9 us)
Sparse Core Ops, SparseCore 0:
  9.6 66.5 all-gather.4
  77.9 25.6 all-gather.6
